TPU v7x, 128 devices: a whole 4x4x4 slice. The times are simulated.
128 devices in a mesh: data: 1, fsdp: 2 (over core), ep: 64 (over z, y, x).
Axes of the slice: x: 4, y: 4, z: 4, core: 2. Of those that a mesh axis runs over, the one named last changes fastest.
Arguments:
- x_in: bfloat16 [384, 512, 768], P(('data', 'fsdp', 'ep'))
- expert_idx: int32 [384, 512, 1], P(('data', 'fsdp', 'ep'))
- expert_slot: int32 [384, 512, 1], P(('data', 'fsdp', 'ep'))
- expert_gate: bfloat16 [384, 512, 1], P(('data', 'fsdp', 'ep'))
- attn_gain: bfloat16 [768], replicated
- w_qkv: bfloat16 [768, 3, 12, 64], P('fsdp')
- w_out: bfloat16 [12, 64, 768], P('fsdp')
- moe_gain: bfloat16 [768], replicated
- w_gate: bfloat16 [64, 768, 3072], P('ep', 'fsdp')
- w_up: bfloat16 [64, 768, 3072], P('ep', 'fsdp')
- w_down: bfloat16 [64, 3072, 768], P('ep', None, 'fsdp')
Outputs:
- output: bfloat16 [384, 512, 768], P(('data', 'fsdp', 'ep'))
All inputs are finite; a program needn't handle non-finite values.
Results may differ from a plain program's by a relative error of at most 0.00933228.
Values are sent between devices in bfloat16 or wider.
A program may use at most 1 GiB of HBM per device.

v0:
```python
import jax
import jax.numpy as jnp
from jax import lax
from jax.sharding import PartitionSpec as P

NORM_EPS = 1e-6
ROPE_BASE = 10000.0


def rms_norm(hidden, gain_vec):
    wide = hidden.astype(jnp.float32)
    inv_rms = lax.rsqrt(jnp.mean(wide * wide, axis=-1, keepdims=True) + NORM_EPS)
    return (wide * inv_rms * gain_vec.astype(jnp.float32)).astype(jnp.bfloat16)


def attention_block(x_blk, attn_gain, w_qkv, w_out):
    seq_len = x_blk.shape[1]
    head_dim = w_qkv.shape[3]
    half_dim = head_dim // 2
    normed = rms_norm(x_blk, attn_gain)
    qkv_proj = jnp.einsum('bsd,dthe->bsthe', normed, w_qkv, preferred_element_type=jnp.float32)
    inv_freq = ROPE_BASE ** (-jnp.arange(half_dim, dtype=jnp.float32) / half_dim)
    angles = jnp.arange(seq_len, dtype=jnp.float32)[:, None] * inv_freq[None, :]
    cos_tab = jnp.cos(angles)[None, :, None, :]
    sin_tab = jnp.sin(angles)[None, :, None, :]

    def rotate(heads_in):
        first_half = heads_in[..., :half_dim]
        second_half = heads_in[..., half_dim:]
        return jnp.concatenate([first_half * cos_tab - second_half * sin_tab, second_half * cos_tab + first_half * sin_tab], axis=-1)

    query_rot = rotate(qkv_proj[:, :, 0]).astype(jnp.bfloat16)
    keys_rot = rotate(qkv_proj[:, :, 1]).astype(jnp.bfloat16)
    values = qkv_proj[:, :, 2].astype(jnp.bfloat16)
    scores = jnp.einsum('bqhe,bkhe->bhqk', query_rot, keys_rot, preferred_element_type=jnp.float32) * (head_dim ** -0.5)
    causal = jnp.arange(seq_len)[:, None] >= jnp.arange(seq_len)[None, :]
    attn_probs = jax.nn.softmax(jnp.where(causal, scores, -1e30), axis=-1).astype(jnp.bfloat16)
    context = jnp.einsum('bhqk,bkhe->bqhe', attn_probs, values, preferred_element_type=jnp.float32).astype(jnp.bfloat16)
    attn_out = jnp.einsum('crif,ife->cre', context, w_out, preferred_element_type=jnp.float32)
    return (x_blk.astype(jnp.float32) + attn_out).astype(jnp.bfloat16)


def capacity_of(tok_count, top_k, experts):
    return 8 * ((5 * tok_count * top_k) // (32 * experts) + 1)


def route_tables(idx_blk, slot_blk, gate_blk, experts, capacity):
    dest_pos = jnp.where(slot_blk >= 0, idx_blk * capacity + slot_blk, -1)
    positions = jnp.arange(experts * capacity)
    slot_match = dest_pos[..., None] == positions
    dispatch = jnp.sum(slot_match, axis=-2).astype(jnp.bfloat16)
    combine = jnp.sum(jnp.where(slot_match, gate_blk[..., None], jnp.zeros((), jnp.bfloat16)), axis=-2)
    return dispatch, combine


def solution(mesh):
    ep_count = mesh.shape['ep']
    tok_spec = P(('data', 'fsdp', 'ep'), None, None)

    def local_step(x_blk, idx_blk, slot_blk, gate_blk, attn_gain, qkv_shard, out_shard, moe_gain, gate_shard, up_shard, down_shard):
        w_qkv = lax.all_gather(qkv_shard, 'fsdp', axis=0, tiled=True)
        w_out = lax.all_gather(out_shard, 'fsdp', axis=0, tiled=True)
        hidden = attention_block(x_blk, attn_gain, w_qkv, w_out)
        w_gate = lax.all_gather(gate_shard, 'fsdp', axis=1, tiled=True)
        w_up = lax.all_gather(up_shard, 'fsdp', axis=1, tiled=True)
        w_down = lax.all_gather(down_shard, 'fsdp', axis=2, tiled=True)
        batch_rows, seq_len, d_model = x_blk.shape
        tok_count = batch_rows * seq_len
        top_k = idx_blk.shape[-1]
        experts = gate_shard.shape[0] * ep_count
        capacity = capacity_of(tok_count, top_k, experts)
        dispatch, combine = route_tables(idx_blk.reshape(tok_count, top_k), slot_blk.reshape(tok_count, top_k), gate_blk.reshape(tok_count, top_k), experts, capacity)
        normed = rms_norm(hidden, moe_gain).reshape(tok_count, d_model)
        send_buf = jnp.einsum('ts,td->sd', dispatch, normed, preferred_element_type=jnp.float32).astype(jnp.bfloat16)
        recv_buf = lax.all_to_all(send_buf.reshape(experts, capacity, d_model), 'ep', 0, 1, tiled=True)
        gate_act = jnp.einsum('ecd,edf->ecf', recv_buf, w_gate, preferred_element_type=jnp.float32)
        up_act = jnp.einsum('ecd,edf->ecf', recv_buf, w_up, preferred_element_type=jnp.float32)
        inner_act = (jax.nn.silu(gate_act) * up_act).astype(jnp.bfloat16)
        expert_out = jnp.einsum('ecf,efd->ecd', inner_act, w_down, preferred_element_type=jnp.float32).astype(jnp.bfloat16)
        back_buf = lax.all_to_all(expert_out, 'ep', 1, 0, tiled=True).reshape(experts * capacity, d_model)
        moe_sum = jnp.dot(combine, back_buf, preferred_element_type=jnp.float32)
        result = hidden.reshape(tok_count, d_model).astype(jnp.float32) + moe_sum
        return result.astype(jnp.bfloat16).reshape(batch_rows, seq_len, d_model)

    return jax.shard_map(local_step, mesh=mesh, in_specs=(tok_spec, tok_spec, tok_spec, tok_spec, P(None), P('fsdp', None, None, None), P('fsdp', None, None), P(None), P('ep', 'fsdp', None), P('ep', 'fsdp', None), P('ep', None, 'fsdp')), out_specs=tok_spec, check_vma=False)
```

profile of v0, /device:TPU:1, one launch (start us, length us, event | category | flops | bytes accessed | tf_op | source)
XLA Modules:
  0.0 319.8 jit_solution(5530774805975726162)
XLA Ops:
  6.5 0.0 copy-start
  6.5 0.0 copy-start.6
  6.5 0.0 copy-start.7
  6.5 0.0 copy-start.3
  6.5 0.0 copy-start.4
  6.5 0.0 all-gather.6.cloned.1.call-start
  6.6 0.7 all-gather.6.cloned.1.call-update
  7.3 0.0 all-gather.8.cloned.1.call-start
  7.3 0.7 all-gather.8.cloned.1.call-update
  8.0 0.0 all-gather.10.cloned.1.call-start
  8.1 0.7 all-gather.10.cloned.1.call-update
  8.8 0.0 all-gather.12.cloned.1.call-start
  8.8 0.5 all-gather.12.cloned.1.call-update
  9.4 0.8 iota_compare_fusion.1
  10.1 0.0 copy-done
  10.1 0.5 fusion.18
  10.7 0.0 copy-done.6
  10.7 1.0 fusion.70
  11.7 0.0 copy-done.7
  11.7 0.0 copy-done.3
  11.7 0.0 copy-done.4
  11.7 16.5 %all-gather.6.cloned.1.call-done = bf16[768,3,12,64]{0,3,2,1:T(8,128)(2,1)} async-done(((bf16[384,3,12,64]{0,3,2,1:T(8,128)(2,1)}), bf16[768,3,12,64]{0,3,2,1:T(8,128)(2,1)}) %all-gather.6.cloned.1.call-update) | async-done | bytes 3538960 | tf_op jit(solution)/shard_map/all_gather | solution.py:61
  28.2 11.0 %fusion.30 = f32[3,512,3,12,64]{1,4,3,2,0:T(8,128)} fusion(bf16[768,3,12,64]{0,3,2,1:T(8,128)(2,1)} %all-gather.6.cloned.1.call-done, bf16[3,512,768]{2,1,0:T(8,128)(2,1)S(1)} %copy-done, f32[768]{0:T(1024)S(1)} %convert_element_type.104, f32[3,512]{1,0:T(4,128)S(1)} %add_rsqrt_fusion.1), kind=kOutput, calls=%fused_computation.39 | convolution fusion | flops 5440536576 | bytes 20063232 | tf_op jit(solution)/shard_map/bsd,dthe->bsthe/dot_general | solution.py:21
  39.2 0.0 copy-start.1
  39.2 0.0 copy-start.2
  39.2 4.9 %slice_bitcast_fusion.1 = (f32[3,512,12,64]{1,3,2,0:T(8,128)S(1)}, f32[3,512,12,64]{1,3,2,0:T(8,128)S(1)}) fusion(f32[3,512,3,12,64]{1,4,3,2,0:T(8,128)} %fusion.30), kind=kLoop, calls=%fused_computation.29 | loop fusion | bytes 18874368 | tf_op jit(solution)/shard_map/squeeze | solution.py:32
  44.1 0.0 copy-done.1
  44.2 0.0 copy-done.2
  44.2 3.0 subtract_convert_fusion.1
  47.2 20.6 %fusion.80 = (f32[3,12,512]{2,1,0:T(8,128)}, f32[3,12,512,512]{2,3,1,0:T(8,128)}) fusion(pred[512,512]{0,1:T(8,128)(4,1)} %iota_compare_fusion.1, bf16[3,512,12,32]{1,3,2,0:T(8,128)(2,1)} %get-tuple-element.11, bf16[3,512,12,32]{1,3,2,0:T(8,128)(2,1)} %get-tuple-element.12, bf16[3,512,12,32]{1,3,2,0:T(8,128)(2,1)} %get-tuple-element.8, ...), kind=kOutput, calls=%fused_computation.79 | convolution fusion | flops 1255145984 | bytes 42803200 | tf_op jit(solution)/shard_map/sub | solution.py:37
  67.8 0.0 all-gather.8.cloned.1.call-done
  67.8 20.0 %multiply_reduce_fusion = (f32[3,512]{1,0:T(4,128)S(1)}, f32[3,512,768]{2,1,0:T(8,128)}) fusion(bf16[12,64,768]{2,1,0:T(8,128)(2,1)} %all-gather.8.cloned.1.call-done, f32[3,12,512,512]{2,3,1,0:T(8,128)} %get-tuple-element.16, f32[3,12,512]{2,1,0:T(8,128)} %get-tuple-element.15, f32[3,512,3,12,64]{1,4,3,2,0:T(8,128)} %fusion.30, ...), kind=kOutput, calls=%fused_computation.38 | convolution fusion | flops 3047029248 | bytes 48470016 | tf_op jit(solution)/shard_map/crif,ife->cre/dot_general | solution.py:39
  87.8 2.8 multiply_convert_fusion.1
  90.6 7.2 %fusion.37 = bf16[2048,768]{1,0:T(8,128)(2,1)} fusion(bf16[1536,768]{1,0:T(8,128)(2,1)S(1)} %bitcast.97, s32[1536]{0:T(1024)S(1)} %select_n.41), kind=kOutput, calls=%fused_computation.42 | convolution fusion | flops 4842848256 | bytes 5511168 | tf_op jit(solution)/shard_map/ts,td->sd/dot_general | solution.py:74
  97.8 10.1 %all-to-all-start = ((bf16[64,32,768]{2,1,0:T(8,128)(2,1)}), bf16[64,32,768]{2,1,0:T(8,128)(2,1)S(1)}, u32[]{:S(2)}, u32[]{:S(2)}) async-start(bf16[64,32,768]{2,1,0:T(8,128)(2,1)} %bitcast.96), calls=%async_computation | async-start | bytes 6291456 | tf_op jit(solution)/shard_map/all_to_all | solution.py:75
  107.9 0.0 all-gather.14.cloned.1.call-start
  108.0 0.5 all-gather.14.cloned.1.call-update
  108.5 0.0 all-gather.10.cloned.1.call-done
  108.5 45.4 %all-to-all-done = bf16[64,32,768]{2,1,0:T(8,128)(2,1)S(1)} async-done(((bf16[64,32,768]{2,1,0:T(8,128)(2,1)}), bf16[64,32,768]{2,1,0:T(8,128)(2,1)S(1)}, u32[]{:S(2)}, u32[]{:S(2)}) %all-to-all-start) | async-done | bytes 3145760 | tf_op jit(solution)/shard_map/all_to_all | solution.py:75
  153.9 15.4 %fusion.25 = f32[2048,3072]{1,0:T(8,128)} fusion(bf16[2048,768]{1,0:T(8,128)(2,1)S(1)} %bitcast.94, bf16[1,768,3072]{2,1,0:T(8,128)(2,1)} %all-gather.10.cloned.1.call-done), kind=kOutput, calls=%fused_computation.33 | convolution fusion | flops 9663676416 | bytes 33030144 | tf_op jit(solution)/shard_map/ecd,edf->ecf/dot_general | solution.py:76
  169.4 0.0 all-gather.12.cloned.1.call-done
  169.4 0.0 all-gather.14.cloned.1.call-done
  169.4 28.9 %fusion.44 = bf16[1,2048,768]{2,1,0:T(8,128)(2,1)} fusion(bf16[1,3072,768]{2,1,0:T(8,128)(2,1)} %all-gather.14.cloned.1.call-done, f32[2048,3072]{1,0:T(8,128)} %fusion.25, bf16[2048,768]{1,0:T(8,128)(2,1)S(1)} %bitcast.95, bf16[1,768,3072]{2,1,0:T(8,128)(2,1)} %all-gather.12.cloned.1.call-done), kind=kOutput, calls=%fused_computation.47 | convolution fusion | flops 19366674432 | bytes 40894464 | tf_op jit(solution)/shard_map/ecf,efd->ecd/dot_general | solution.py:79
  198.2 6.9 %copy.30 = bf16[1,2048,768]{2,0,1:T(2,128)(2,1)} copy(bf16[1,2048,768]{2,1,0:T(8,128)(2,1)} %fusion.44) | data formatting | bytes 6291456 | tf_op jit(solution)/shard_map/convert_element_type | solution.py:79
  205.1 0.5 broadcast.173
  205.7 31.8 %reduce.2 = bf16[2048,768]{1,0:T(8,128)(2,1)S(1)} reduce(bf16[2048,1,768]{2,1,0:T(2,128)(2,1)} %bitcast.92, bf16[]{:T(256)} %broadcast.173), dimensions={1}, to_apply=%bitcast.91.reduce_sub_computation | reduce | bytes 6291458
  237.5 2.4 reshape.285
  239.9 0.0 copy-start.5
  239.9 8.6 %all-to-all-start.1 = ((bf16[64,2,12288]{2,1,0:T(2,128)(2,1)}), bf16[64,2,12288]{2,1,0:T(2,128)(2,1)S(1)}, u32[]{:S(2)}, u32[]{:S(2)}) async-start(bf16[64,2,12288]{2,1,0:T(2,128)(2,1)} %reshape.285), calls=%async_computation.1 | async-start | bytes 6291456 | tf_op jit(solution)/shard_map/all_to_all | solution.py:80
  248.5 0.0 copy-done.5
  248.6 46.7 %all-to-all-done.1 = bf16[64,2,12288]{2,1,0:T(2,128)(2,1)S(1)} async-done(((bf16[64,2,12288]{2,1,0:T(2,128)(2,1)}), bf16[64,2,12288]{2,1,0:T(2,128)(2,1)S(1)}, u32[]{:S(2)}, u32[]{:S(2)}) %all-to-all-start.1) | async-done | bytes 3145760 | tf_op jit(solution)/shard_map/all_to_all | solution.py:80
  295.3 7.7 %reshape.286 = bf16[2048,1,768]{2,1,0:T(2,128)(2,1)} reshape(bf16[64,2,12288]{2,1,0:T(2,128)(2,1)S(1)} %all-to-all-done.1) | data formatting | bytes 6291456
  303.0 10.3 %fusion.27 = bf16[1536,768]{1,0:T(8,128)(2,1)} fusion(f32[3,512,768]{2,1,0:T(8,128)} %get-tuple-element.18, s32[1536]{0:T(1024)S(1)} %select_n.41, bf16[1,2048,768]{2,0,1:T(2,128)(2,1)} %bitcast.93, bf16[1536]{0:T(1024)(128)(2,1)S(1)} %broadcast_in_dim.43), kind=kOutput, calls=%fused_computation.36 | convolution fusion | flops 4840488960 | bytes 10232832 | tf_op jit(solution)/shard_map/dot_general | solution.py:81
  (8 shorter events, 0.1 us)
Async XLA Ops:
  6.5 3.6 %copy-start = (bf16[3,512,768]{2,1,0:T(8,128)(2,1)S(1)}, bf16[3,512,768]{2,1,0:T(8,128)(2,1)}, u32[]{:S(2)}) copy-start(bf16[3,512,768]{2,1,0:T(8,128)(2,1)} %param.11) | copy-start | bytes 7077892
  6.5 4.2 %copy-start.6 = (bf16[768]{0:T(1024)(128)(2,1)S(1)}, bf16[768]{0:T(1024)(128)(2,1)}, u32[]{:S(2)}) copy-start(bf16[768]{0:T(1024)(128)(2,1)} %param.15) | copy-start | bytes 4612
  6.5 5.1 %copy-start.7 = (bf16[768]{0:T(1024)(128)(2,1)S(1)}, bf16[768]{0:T(1024)(128)(2,1)}, u32[]{:S(2)}) copy-start(bf16[768]{0:T(1024)(128)(2,1)} %param.18) | copy-start | bytes 4612
  6.5 5.1 %copy-start.3 = (s32[3,512,1]{1,2,0:T(1,128)S(1)}, s32[3,512,1]{1,2,0:T(1,128)}, u32[]{:S(2)}) copy-start(s32[3,512,1]{1,2,0:T(1,128)} %param.13) | copy-start | bytes 18436
  6.5 5.1 %copy-start.4 = (s32[3,512,1]{1,2,0:T(1,128)S(1)}, s32[3,512,1]{1,2,0:T(1,128)}, u32[]{:S(2)}) copy-start(s32[3,512,1]{1,2,0:T(1,128)} %param.12) | copy-start | bytes 18436
  6.5 21.7 %all-gather.6.cloned.1.call-start = ((), (), s32[]{:S(2)}) async-start(), calls=%async_computation.2 | async-start | bytes 5308416 | tf_op jit(solution)/shard_map/all_gather | solution.py:61
  7.3 60.5 %all-gather.8.cloned.1.call-start = ((), (), s32[]{:S(2)}) async-start(), calls=%async_computation.3 | async-start | bytes 1769472 | tf_op jit(solution)/shard_map/all_gather | solution.py:62
  8.0 100.5 %all-gather.10.cloned.1.call-start = ((), (), s32[]{:S(2)}) async-start(), calls=%async_computation.4 | async-start | bytes 7077888 | tf_op jit(solution)/shard_map/all_gather | solution.py:64
  8.8 160.6 %all-gather.12.cloned.1.call-start = ((), (), s32[]{:S(2)}) async-start(), calls=%async_computation.5 | async-start | bytes 7077888 | tf_op jit(solution)/shard_map/all_gather | solution.py:65
  39.2 4.9 %copy-start.1 = (f32[512,32]{0,1:T(8,128)S(1)}, f32[512,32]{0,1:T(8,128)}, u32[]{:S(2)}) copy-start(f32[512,32]{0,1:T(8,128)} %get-tuple-element.13) | copy-start | bytes 196612
  39.2 4.9 %copy-start.2 = (f32[512,32]{0,1:T(8,128)S(1)}, f32[512,32]{0,1:T(8,128)}, u32[]{:S(2)}) copy-start(f32[512,32]{0,1:T(8,128)} %get-tuple-element.14) | copy-start | bytes 196612
  97.8 56.1 %all-to-all-start = ((bf16[64,32,768]{2,1,0:T(8,128)(2,1)}), bf16[64,32,768]{2,1,0:T(8,128)(2,1)S(1)}, u32[]{:S(2)}, u32[]{:S(2)}) async-start(bf16[64,32,768]{2,1,0:T(8,128)(2,1)} %bitcast.96), calls=%async_computation | async-start | bytes 6291456 | tf_op jit(solution)/shard_map/all_to_all | solution.py:75
  107.9 61.4 %all-gather.14.cloned.1.call-start = ((), (), s32[]{:S(2)}) async-start(), calls=%async_computation.6 | async-start | bytes 7077888 | tf_op jit(solution)/shard_map/all_gather | solution.py:66
  239.9 8.6 %copy-start.5 = (bf16[3,512,1]{1,0,2:T(4,128)(2,1)S(1)}, bf16[3,512,1]{1,0,2:T(4,128)(2,1)}, u32[]{:S(2)}) copy-start(bf16[3,512,1]{1,0,2:T(4,128)(2,1)} %param.14) | copy-start | bytes 9220
  239.9 55.4 %all-to-all-start.1 = ((bf16[64,2,12288]{2,1,0:T(2,128)(2,1)}), bf16[64,2,12288]{2,1,0:T(2,128)(2,1)S(1)}, u32[]{:S(2)}, u32[]{:S(2)}) async-start(bf16[64,2,12288]{2,1,0:T(2,128)(2,1)} %reshape.285), calls=%async_computation.1 | async-start | bytes 6291456 | tf_op jit(solution)/shard_map/all_to_all | solution.py:80
Sparse Core Ops, SparseCore 0:
  9.0 19.1 all-gather.5
  29.9 13.1 all-gather.7
  44.7 18.8 all-gather.9
  65.1 18.8 all-gather.11
  110.1 18.9 all-gather.13
where the time goes:
time: 320 us
  matrix products  113 us (35%)
  waiting for transfers between devices  112 us (35%)
  other arithmetic  40 us (12%)
  local copies, waits for them, and re-layouts  22.5 us (7%)
  starting transfers between devices  18.9 us (6%)
  between operations  13.3 us (4%)
    all_to_all x1, waiting for transfers between devices, local_step(): lax.all_to_all(expert_out, 'ep', 1, 0, tiled=True)  46.7 us
    all_to_all x1, waiting for transfers between devices, local_step(): lax.all_to_all(send_buf.reshape(experts, capacity, d_model), 'ep', 0, 1,...  45.4 us
    unnamed x1, other arithmetic  31.8 us
    dot_general x1, matrix products, local_step(): jnp.einsum('ecf,efd->ecd', inner_act, w_down, preferred_element_type=jnp....  28.9 us
    sub x1, matrix products, attention_block(): jax.nn.softmax(jnp.where(causal, scores, -1e+30), axis=-1)  20.6 us
    dot_general x1, matrix products, attention_block(): jnp.einsum('crif,ife->cre', context, w_out, preferred_element_type=jnp.fl...  20 us
    all_gather x1, waiting for transfers between devices, local_step(): w_qkv = lax.all_gather(qkv_shard, 'fsdp', axis=0, tiled=True)  16.5 us
    dot_general x1, matrix products, local_step(): jnp.einsum('ecd,edf->ecf', recv_buf, w_gate, preferred_element_type=jnp.f...  15.4 us
  transfers between devices with their start and end apart: 7, of which 3 were waited for; matrix products, arithmetic and copies ran while one was open for 27% of the time, Pallas kernels for 0%

commit v1 on v0

v1 whole, which is shorter than its diff:
```python
import functools

import jax
import jax.numpy as jnp
from jax import lax
from jax.experimental import pallas as pl
from jax.experimental.pallas import tpu as pltpu
from jax.sharding import PartitionSpec as P

MESH = pl.DeviceIdType.MESH
NORM_EPS = 1e-6
ROPE_BASE = 10000.0
N_EP = 64
CAP = 32
GROUP = 8
GROWS = GROUP * CAP
N_GROUPS = N_EP // GROUP
TOK = 1536
TTILE = 512
FFN = 3072
FTILE = 512


def rms_norm(hidden, gain_vec):
    wide = hidden.astype(jnp.float32)
    inv_rms = lax.rsqrt(jnp.mean(wide * wide, axis=-1, keepdims=True) + NORM_EPS)
    return (wide * inv_rms * gain_vec.astype(jnp.float32)).astype(jnp.bfloat16)


def attention_block(x_blk, attn_gain, w_qkv, w_out):
    seq_len = x_blk.shape[1]
    head_dim = w_qkv.shape[3]
    half_dim = head_dim // 2
    normed = rms_norm(x_blk, attn_gain)
    qkv_proj = jnp.einsum('bsd,dthe->bsthe', normed, w_qkv, preferred_element_type=jnp.float32)
    inv_freq = ROPE_BASE ** (-jnp.arange(half_dim, dtype=jnp.float32) / half_dim)
    angles = jnp.arange(seq_len, dtype=jnp.float32)[:, None] * inv_freq[None, :]
    cos_tab = jnp.cos(angles)[None, :, None, :]
    sin_tab = jnp.sin(angles)[None, :, None, :]

    def rotate(heads_in):
        first_half = heads_in[..., :half_dim]
        second_half = heads_in[..., half_dim:]
        return jnp.concatenate([first_half * cos_tab - second_half * sin_tab, second_half * cos_tab + first_half * sin_tab], axis=-1)

    query_rot = rotate(qkv_proj[:, :, 0]).astype(jnp.bfloat16)
    keys_rot = rotate(qkv_proj[:, :, 1]).astype(jnp.bfloat16)
    values = qkv_proj[:, :, 2].astype(jnp.bfloat16)
    scores = jnp.einsum('bqhe,bkhe->bhqk', query_rot, keys_rot, preferred_element_type=jnp.float32) * (head_dim ** -0.5)
    causal = jnp.arange(seq_len)[:, None] >= jnp.arange(seq_len)[None, :]
    attn_probs = jax.nn.softmax(jnp.where(causal, scores, -1e30), axis=-1).astype(jnp.bfloat16)
    context = jnp.einsum('bhqk,bkhe->bqhe', attn_probs, values, preferred_element_type=jnp.float32).astype(jnp.bfloat16)
    attn_out = jnp.einsum('crif,ife->cre', context, w_out, preferred_element_type=jnp.float32)
    return (x_blk.astype(jnp.float32) + attn_out).astype(jnp.bfloat16)


def moe_kernel(u_ref, h_ref, drow_ref, dcol_ref, gcol_ref, wg_hbm, wu_hbm, wd_hbm, out_ref,
               send, recv, ybuf, back, wg, wu, wd, act, acc,
               w_local, w_send, w_recv, out_send, out_recv, ret_send, ret_recv):
    fs = lax.axis_index('fsdp')
    ep = lax.axis_index('ep')
    me = (lax.rem(ep, 4), lax.rem(ep // 4, 4), ep // 16)
    half = wg_hbm.shape[1]

    def peer(k, sign):
        offs = (lax.rem(k, 4), lax.rem(k // 4, 4), k // 16)
        px, py, pz = [lax.rem(m + sign * o + 4, 4) for m, o in zip(me, offs)]
        return pz * 16 + py * 4 + px

    def slot_ids(k_of_row, c_of_row):
        ex = (me[0] + k_of_row) & 3
        ey = (me[1] + (k_of_row >> 2)) & 3
        ez = (me[2] + (k_of_row >> 4)) & 3
        return (ez * 16 + ey * 4 + ex) * CAP + c_of_row

    barrier = pltpu.get_barrier_semaphore()
    pl.semaphore_signal(barrier, inc=1, device_id=(0, 1 - fs, ep), device_id_type=MESH)

    @pl.loop(1, N_EP)
    def _(k):
        pl.semaphore_signal(barrier, inc=1, device_id=(0, fs, peer(k, 1)), device_id_type=MESH)

    lo = pl.multiple_of(fs * half, half)
    weight_views = (
        (wg_hbm.at[0], wg.at[pl.ds(lo, half)]),
        (wu_hbm.at[0], wu.at[pl.ds(lo, half)]),
        (wd_hbm.at[0], wd.at[:, pl.ds(lo, half)]),
    )
    local_copies = [pltpu.make_async_copy(src, dst, w_local.at[i]) for i, (src, dst) in enumerate(weight_views)]
    remote_copies = [
        pltpu.make_async_remote_copy(src_ref=src, dst_ref=dst, send_sem=w_send.at[i], recv_sem=w_recv.at[i], device_id=(0, 1 - fs, ep), device_id_type=MESH)
        for i, (src, dst) in enumerate(weight_views)
    ]
    for copy in local_copies:
        copy.start()
    pl.semaphore_wait(barrier, N_EP)
    for copy in remote_copies:
        copy.start()

    def out_copy(k):
        rows = pl.ds(pl.multiple_of(k * CAP, CAP), CAP)
        return pltpu.make_async_remote_copy(
            src_ref=send.at[rows], dst_ref=recv.at[rows], send_sem=out_send.at[k], recv_sem=out_recv.at[k],
            device_id=(0, fs, peer(k, 1)), device_id_type=MESH)

    def ret_copy(k):
        rows = pl.ds(pl.multiple_of(k * CAP, CAP), CAP)
        return pltpu.make_async_remote_copy(
            src_ref=ybuf.at[rows], dst_ref=back.at[rows], send_sem=ret_send.at[k], recv_sem=ret_recv.at[k],
            device_id=(0, fs, peer(k, -1)), device_id_type=MESH)

    def each(g, act_on):
        for j in range(GROUP):
            k = g * GROUP + j
            if j == 0:
                pl.when(k > 0)(functools.partial(act_on, k))
            else:
                act_on(k)

    @pl.loop(0, N_GROUPS)
    def _(g):
        row = lax.broadcasted_iota(jnp.int32, (GROWS, 1), 0)
        sid = slot_ids(g * GROUP + (row >> 5), row & (CAP - 1))
        pick = jnp.where(sid == drow_ref[...], 1.0, 0.0).astype(jnp.bfloat16)
        rows = jnp.dot(pick, u_ref[...], preferred_element_type=jnp.float32)
        send[pl.ds(pl.multiple_of(g * GROWS, GROWS), GROWS)] = rows.astype(jnp.bfloat16)
        each(g, lambda k: out_copy(k).start())

    recv[pl.ds(0, CAP)] = send[pl.ds(0, CAP)]
    for copy in local_copies:
        copy.wait()
    for copy in remote_copies:
        copy.wait_recv()

    @pl.loop(0, N_GROUPS)
    def _(g):
        each(g, lambda k: out_copy(k).wait_recv())
        here = pl.ds(pl.multiple_of(g * GROWS, GROWS), GROWS)

        @pl.loop(0, FFN // FTILE)
        def _(t):
            cols = pl.ds(pl.multiple_of(t * FTILE, FTILE), FTILE)
            gate_act = jnp.dot(recv[here], wg[:, cols], preferred_element_type=jnp.float32)
            up_act = jnp.dot(recv[here], wu[:, cols], preferred_element_type=jnp.float32)
            act[:, cols] = (jax.nn.silu(gate_act) * up_act).astype(jnp.bfloat16)

        ybuf[here] = jnp.dot(act[...], wd[...], preferred_element_type=jnp.float32).astype(jnp.bfloat16)
        each(g, lambda k: ret_copy(k).start())

    back[pl.ds(0, CAP)] = ybuf[pl.ds(0, CAP)]

    def combine(g, first, last):
        each(g, lambda k: ret_copy(k).wait_recv())
        col = lax.broadcasted_iota(jnp.int32, (1, GROWS), 1)
        sid = slot_ids(g * GROUP + (col >> 5), col & (CAP - 1))

        @pl.loop(0, TOK // TTILE)
        def _(i):
            toks = pl.ds(pl.multiple_of(i * TTILE, TTILE), TTILE)
            pick = jnp.where(sid == dcol_ref[toks], gcol_ref[toks], 0.0).astype(jnp.bfloat16)
            part = jnp.dot(pick, back[pl.ds(pl.multiple_of(g * GROWS, GROWS), GROWS)], preferred_element_type=jnp.float32)
            prev = h_ref[toks].astype(jnp.float32) if first else acc[toks]
            if last:
                out_ref[toks] = (prev + part).astype(jnp.bfloat16)
            else:
                acc[toks] = prev + part

    combine(0, True, False)

    @pl.loop(1, N_GROUPS - 1)
    def _(g):
        combine(g, False, False)

    combine(N_GROUPS - 1, False, True)

    for copy in remote_copies:
        copy.wait_send()

    @pl.loop(1, N_EP)
    def _(k):
        out_copy(k).wait_send()
        ret_copy(k).wait_send()


def moe(u, h, dest, gate, wg, wu, wd):
    vmem = pl.BlockSpec(memory_space=pltpu.VMEM)
    hbm = pl.BlockSpec(memory_space=pl.ANY)
    slots, d = N_EP * CAP, u.shape[1]
    dma = pltpu.SemaphoreType.DMA
    return pl.pallas_call(
        moe_kernel,
        out_shape=jax.ShapeDtypeStruct(u.shape, jnp.bfloat16),
        in_specs=[vmem] * 5 + [hbm] * 3,
        out_specs=vmem,
        scratch_shapes=[pltpu.VMEM((slots, d), jnp.bfloat16)] * 4 + [
            pltpu.VMEM((d, FFN), jnp.bfloat16), pltpu.VMEM((d, FFN), jnp.bfloat16), pltpu.VMEM((FFN, d), jnp.bfloat16),
            pltpu.VMEM((GROWS, FFN), jnp.bfloat16), pltpu.VMEM((TOK, d), jnp.float32),
            dma((3,)), dma((3,)), dma((3,)), dma((N_EP,)), dma((N_EP,)), dma((N_EP,)), dma((N_EP,))],
        compiler_params=pltpu.CompilerParams(collective_id=1, has_side_effects=True, vmem_limit_bytes=60 << 20),
        name='moe',
    )(u, h, dest.reshape(1, TOK), dest.reshape(TOK, 1), gate.reshape(TOK, 1), wg, wu, wd)


def solution(mesh):
    tok_spec = P(('data', 'fsdp', 'ep'), None, None)

    def local_step(x_blk, idx_blk, slot_blk, gate_blk, attn_gain, qkv_shard, out_shard, moe_gain, gate_shard, up_shard, down_shard):
        w_qkv = lax.all_gather(qkv_shard, 'fsdp', axis=0, tiled=True)
        w_out = lax.all_gather(out_shard, 'fsdp', axis=0, tiled=True)
        hidden = attention_block(x_blk, attn_gain, w_qkv, w_out)
        batch_rows, seq_len, d_model = x_blk.shape
        dest = jnp.where(slot_blk >= 0, idx_blk * CAP + slot_blk, -1).reshape(TOK)
        normed = rms_norm(hidden, moe_gain).reshape(TOK, d_model)
        result = moe(normed, hidden.reshape(TOK, d_model), dest, gate_blk.astype(jnp.float32), gate_shard, up_shard, down_shard)
        return result.reshape(batch_rows, seq_len, d_model)

    return jax.shard_map(local_step, mesh=mesh, in_specs=(tok_spec, tok_spec, tok_spec, tok_spec, P(None), P('fsdp', None, None, None), P('fsdp', None, None), P(None), P('ep', 'fsdp', None), P('ep', 'fsdp', None), P('ep', None, 'fsdp')), out_specs=tok_spec, check_vma=False)
```

time: 320 us -> 212 us (0.66); the launches traced: 320 us -> 208 us
  Pallas kernels: 0 us -> 110 us
  waiting for transfers between devices: 112 us -> 16.8 us
  matrix products: 113 us -> 49.7 us
  other arithmetic: 40 us -> 7.07 us
  starting transfers between devices: 18.9 us -> 0.08 us
  local copies, waits for them, and re-layouts: 22.5 us -> 10.6 us
    pallas_call x0 -> x1, Pallas kernels: none -> 110 us  [moe(): pl.pallas_call(moe_kernel, out_shape=jax.ShapeDtypeStruct(u.shape, jnp.bf...]
    all_to_all x2 -> x0, waiting for transfers between devices: 92.1 us -> none  [the longest x1 46.7 us: local_step(): lax.all_to_all(expert_out, 'ep', 1, 0, tiled=True)]
    dot_general x4 -> x0, matrix products: 61.8 us -> none  [the longest x1 28.9 us: local_step(): jnp.einsum('ecf,efd->ecd', inner_act, w_down, preferred_element_type=jnp....]
    unnamed x1, other arithmetic: 31.8 us -> 0.01 us
    all_to_all x2 -> x0, starting transfers between devices: 18.7 us -> none  [the longest x1 10.1 us: local_step(): lax.all_to_all(send_buf.reshape(experts, capacity, d_model), 'ep', 0, 1,...]
    convert_element_type x1 -> x0, local copies, waits for them, and re-layouts: 6.91 us -> none  [local_step(): jnp.einsum('ecf,efd->ecd', inner_act, w_down, preferred_element_type=jnp....]
    unnamed x19 -> x23, local copies, waits for them, and re-layouts: 10.7 us -> 4.48 us
  transfers between devices with their start and end apart: 7 -> 2, of which waited for: 3 -> 1; matrix products, arithmetic and copies ran while one was open for 27% -> 21% of each run, Pallas kernels for 0% -> 0%
where the time goes in v1:
time: 212 us; the launch traced here: 208 us
  Pallas kernels  110 us (52%)
  matrix products  49.7 us (23%)
  waiting for transfers between devices  16.8 us (8%)
  between operations  13.5 us (6%)
  local copies, waits for them, and re-layouts  10.6 us (5%)
  other arithmetic  7.07 us (3%)
    pallas_call x1, Pallas kernels, moe(): pl.pallas_call(moe_kernel, out_shape=jax.ShapeDtypeStruct(u.shape, jnp.bf...  110 us
    sub x1, matrix products, attention_block(): jax.nn.softmax(jnp.where(causal, scores, -1e+30), axis=-1)  20.3 us
    dot_general x1, matrix products, attention_block(): jnp.einsum('crif,ife->cre', context, w_out, preferred_element_type=jnp.fl...  18.4 us
    all_gather x1, waiting for transfers between devices, local_step(): w_qkv = lax.all_gather(qkv_shard, 'fsdp', axis=0, tiled=True)  15.4 us
    dot_general x1, matrix products, attention_block(): jnp.einsum('bsd,dthe->bsthe', normed, w_qkv, preferred_element_type=jnp.f...  11 us
    squeeze x1, local copies, waits for them, and re-layouts, attention_block(): query_rot = rotate(qkv_proj[:, :, 0]).astype(jnp.bfloat16)  4.92 us
    unnamed x23, local copies, waits for them, and re-layouts  4.48 us
  transfers between devices with their start and end apart: 2, of which 1 were waited for; matrix products, arithmetic and copies ran while one was open for 21% of the time, Pallas kernels for 0%

profile of v1, /device:TPU:1, one launch (start us, length us, event | category | flops | bytes accessed | tf_op | source)
XLA Modules:
  0.0 208.0 jit_solution(18176574013368923181)
XLA Ops:
  6.5 0.0 copy-start.1
  6.5 0.0 copy-start.8
  6.5 0.0 copy-start.9
  6.5 0.0 copy-start.6
  6.5 0.0 copy-start.5
  6.5 0.0 all-gather.3.cloned.1.call-start
  6.6 0.7 all-gather.3.cloned.1.call-update
  7.3 0.0 copy-start.7
  7.3 0.0 all-gather.5.cloned.1.call-start
  7.3 0.7 all-gather.5.cloned.1.call-update
  8.1 0.8 iota_compare_fusion
  8.8 0.0 copy-done.1
  8.8 0.5 fusion.11
  9.4 0.0 copy-done.8
  9.4 1.0 fusion.37
  10.4 0.0 copy-done.9
  10.4 0.0 copy-done.6
  10.4 0.0 copy-done.5
  10.4 0.0 copy-start.4
  10.4 1.2 copy.18.dcol_ref
  11.6 0.0 copy-done.7
  11.6 1.2 copy.25
  12.8 15.4 %all-gather.3.cloned.1.call-done = bf16[768,3,12,64]{0,3,2,1:T(8,128)(2,1)} async-done(((bf16[384,3,12,64]{0,3,2,1:T(8,128)(2,1)}), bf16[768,3,12,64]{0,3,2,1:T(8,128)(2,1)}) %all-gather.3.cloned.1.call-update) | async-done | bytes 3538960 | tf_op jit(solution)/shard_map/all_gather | solution.py:208
  28.2 11.0 %fusion.15 = f32[3,512,3,12,64]{1,4,3,2,0:T(8,128)} fusion(bf16[768,3,12,64]{0,3,2,1:T(8,128)(2,1)} %all-gather.3.cloned.1.call-done, bf16[3,512,768]{2,1,0:T(8,128)(2,1)S(1)} %copy-done.1, f32[768]{0:T(1024)S(1)} %convert_element_type.39, f32[3,512]{1,0:T(4,128)S(1)} %add_rsqrt_fusion.1), kind=kOutput, calls=%fused_computation.25 | convolution fusion | flops 5440536576 | bytes 20063232 | tf_op jit(solution)/shard_map/bsd,dthe->bsthe/dot_general | solution.py:35
  39.2 0.0 copy-done.4
  39.2 0.0 copy-start.2
  39.2 0.0 copy-start.3
  39.2 4.9 %slice_bitcast_fusion.1 = (f32[3,512,12,64]{1,3,2,0:T(8,128)S(1)}, f32[3,512,12,64]{1,3,2,0:T(8,128)S(1)}) fusion(f32[3,512,3,12,64]{1,4,3,2,0:T(8,128)} %fusion.15), kind=kLoop, calls=%fused_computation.23 | loop fusion | bytes 18874368 | tf_op jit(solution)/shard_map/squeeze | solution.py:46
  44.1 0.0 copy-done.2
  44.1 0.0 copy-done.3
  44.2 2.6 %subtract_convert_fusion.1 = (bf16[3,512,12,32]{1,3,2,0:T(8,128)(2,1)S(1)}, bf16[3,512,12,32]{1,3,2,0:T(8,128)(2,1)S(1)}, bf16[3,512,12,32]{1,3,2,0:T(8,128)(2,1)S(1)}, bf16[3,512,12,32]{1,3,2,0:T(8,128)(2,1)}) fusion(f32[3,512,12,64]{1,3,2,0:T(8,128)S(1)} %get-tuple-element.5, f32[512,32]{0,1:T(8,128)S(1)} %copy-done.3, f32[512,32]{0,1:T(8,128)S(1)} %copy-done.2, ...), kind=kLoop, calls=%fused_computation.37 | loop fusion | flops 9437184 | bytes 14286848 | tf_op jit(solution)/shard_map/convert.3
  46.7 20.3 %fusion.44 = (f32[3,12,512]{2,1,0:T(8,128)}, f32[3,12,512,512]{2,3,1,0:T(8,128)}) fusion(pred[512,512]{0,1:T(8,128)(4,1)} %iota_compare_fusion, bf16[3,512,12,32]{1,3,2,0:T(8,128)(2,1)S(1)} %get-tuple-element.11, bf16[3,512,12,32]{1,3,2,0:T(8,128)(2,1)} %get-tuple-element.12, bf16[3,512,12,32]{1,3,2,0:T(8,128)(2,1)S(1)} %get-tuple-element.8, ...), kind=kOutput, calls=%fused_computation.55 | convolution fusion | flops 1255145984 | bytes 42803200 | tf_op jit(solution)/shard_map/sub | solution.py:51
  67.1 0.0 all-gather.5.cloned.1.call-done
  67.1 18.4 %fusion.8 = (f32[3,512]{1,0:T(4,128)S(1)}, bf16[3,512,768]{2,1,0:T(8,128)(2,1)S(1)}) fusion(bf16[12,64,768]{2,1,0:T(8,128)(2,1)} %all-gather.5.cloned.1.call-done, f32[3,12,512,512]{2,3,1,0:T(8,128)} %get-tuple-element.16, f32[3,12,512]{2,1,0:T(8,128)} %get-tuple-element.15, f32[3,512,3,12,64]{1,4,3,2,0:T(8,128)} %fusion.15, bf16[3,512,768]{2,1,0:T(8,128)(2,1)} %param.11), kind=kOutput, calls=%fused_computation.15 | convolution fusion | flops 3047029248 | bytes 46110720 | tf_op jit(solution)/shard_map/crif,ife->cre/dot_general | solution.py:53
  85.5 0.0 copy-start
  85.5 2.2 %fusion.10 = bf16[3,512,768]{2,1,0:T(8,128)(2,1)} fusion(bf16[3,512,768]{2,1,0:T(8,128)(2,1)S(1)} %get-tuple-element.18, f32[768]{0:T(1024)S(1)} %convert_element_type.47, f32[3,512]{1,0:T(4,128)S(1)} %add_rsqrt_fusion), kind=kLoop, calls=%fused_computation.17 | loop fusion | flops 4718592 | bytes 4727808 | tf_op jit(solution)/shard_map/convert_element_type | solution.py:27
  87.6 0.0 copy-done
  87.6 110.3 %moe.1 = bf16[1536,768]{1,0:T(8,128)(2,1)} custom-call(bf16[1536,768]{1,0:T(8,128)(2,1)} %bitcast.51, bf16[1536,768]{1,0:T(8,128)(2,1)} %bitcast.50, s32[1,1536]{1,0:T(1,128)} %bitcast.55, s32[1536,1]{1,0:T(8,128)} %copy.18.dcol_ref, f32[1536,1]{1,0:T(8,128)} %bitcast.53, bf16[1,384,3072]{2,1,0:T(8,128)(2,1)} %wg_hbm.1, bf16[1,384,3072]{2,1,0:T(8,128)(2,1)} %wu_hbm.1, ...), custom_call_target="tpu_custom_call" | custom-call | tf_op jit(solution)/shard_map/moe/pallas_call | solution.py:190
  197.9 3.2 %copy.27 = bf16[3,512,768]{2,1,0:T(8,128)(2,1)} copy(bf16[3,512,768]{2,1,0:T(8,128)(2,1)} %bitcast.52) | data formatting | bytes 4718592
  (8 shorter events, 0.1 us)
Async XLA Ops:
  6.5 2.3 %copy-start.1 = (bf16[3,512,768]{2,1,0:T(8,128)(2,1)S(1)}, bf16[3,512,768]{2,1,0:T(8,128)(2,1)}, u32[]{:S(2)}) copy-start(bf16[3,512,768]{2,1,0:T(8,128)(2,1)} %param.11) | copy-start | bytes 7077892
  6.5 2.9 %copy-start.8 = (bf16[768]{0:T(1024)(128)(2,1)S(1)}, bf16[768]{0:T(1024)(128)(2,1)}, u32[]{:S(2)}) copy-start(bf16[768]{0:T(1024)(128)(2,1)} %param.15) | copy-start | bytes 4612
  6.5 3.8 %copy-start.9 = (bf16[768]{0:T(1024)(128)(2,1)S(1)}, bf16[768]{0:T(1024)(128)(2,1)}, u32[]{:S(2)}) copy-start(bf16[768]{0:T(1024)(128)(2,1)} %param.18) | copy-start | bytes 4612
  6.5 3.8 %copy-start.6 = (s32[3,512,1]{1,2,0:T(1,128)S(1)}, s32[3,512,1]{1,2,0:T(1,128)}, u32[]{:S(2)}) copy-start(s32[3,512,1]{1,2,0:T(1,128)} %param.12) | copy-start | bytes 18436
  6.5 3.8 %copy-start.5 = (s32[3,512,1]{1,2,0:T(1,128)S(1)}, s32[3,512,1]{1,2,0:T(1,128)}, u32[]{:S(2)}) copy-start(s32[3,512,1]{1,2,0:T(1,128)} %param.13) | copy-start | bytes 18436
  6.5 21.7 %all-gather.3.cloned.1.call-start = ((), (), s32[]{:S(2)}) async-start(), calls=%async_computation | async-start | bytes 5308416 | tf_op jit(solution)/shard_map/all_gather | solution.py:208
  7.3 4.3 %copy-start.7 = (bf16[3,512,1]{1,0,2:T(4,128)(2,1)S(1)}, bf16[3,512,1]{1,0,2:T(4,128)(2,1)}, u32[]{:S(2)}) copy-start(bf16[3,512,1]{1,0,2:T(4,128)(2,1)} %param.14) | copy-start | bytes 9220
  7.3 59.8 %all-gather.5.cloned.1.call-start = ((), (), s32[]{:S(2)}) async-start(), calls=%async_computation.1 | async-start | bytes 1769472 | tf_op jit(solution)/shard_map/all_gather | solution.py:209
  10.4 28.8 %copy-start.4 = (s32[3,512,1]{1,2,0:T(1,128)}, s32[3,512,1]{1,2,0:T(1,128)S(1)}, u32[]{:S(2)}) copy-start(s32[3,512,1]{1,2,0:T(1,128)S(1)} %compare_select_fusion) | copy-start | bytes 18436
  39.2 4.9 %copy-start.2 = (f32[512,32]{0,1:T(8,128)S(1)}, f32[512,32]{0,1:T(8,128)}, u32[]{:S(2)}) copy-start(f32[512,32]{0,1:T(8,128)} %get-tuple-element.13) | copy-start | bytes 196612
  39.2 4.9 %copy-start.3 = (f32[512,32]{0,1:T(8,128)S(1)}, f32[512,32]{0,1:T(8,128)}, u32[]{:S(2)}) copy-start(f32[512,32]{0,1:T(8,128)} %get-tuple-element.14) | copy-start | bytes 196612
  85.5 2.2 %copy-start = (bf16[3,512,768]{2,1,0:T(8,128)(2,1)}, bf16[3,512,768]{2,1,0:T(8,128)(2,1)S(1)}, u32[]{:S(2)}) copy-start(bf16[3,512,768]{2,1,0:T(8,128)(2,1)S(1)} %get-tuple-element.18) | copy-start | bytes 7077892
Sparse Core Ops, SparseCore 0:
  9.0 19.1 all-gather.2
  29.9 13.1 all-gather.4

commit v2 on v1

v2 whole, which is shorter than its diff:
```python
import functools

import jax
import jax.numpy as jnp
import numpy as np
from jax import lax
from jax.experimental import pallas as pl
from jax.experimental.pallas import tpu as pltpu
from jax.sharding import PartitionSpec as P

MESH = pl.DeviceIdType.MESH
NORM_EPS = 1e-6
ROPE_BASE = 10000.0
N_EP = 64
CAP = 32
GROUP = 8
GROWS = GROUP * CAP
N_GROUPS = N_EP // GROUP
SEQS = 3
SEQ = 512
TOK = SEQS * SEQ
TTILE = 512
D = 768
FFN = 3072
FTILE = 512
HEADS = 12
HEAD = 64
QKV = 3 * HEADS * HEAD
QTILE = 256
LANES = 128
F32, BF16 = jnp.float32, jnp.bfloat16


def rows_at(i, size):
    return pl.ds(pl.multiple_of(i * size, size), size)


def norm(wide, gain):
    inv_rms = lax.rsqrt(jnp.mean(wide * wide, axis=-1, keepdims=True) + NORM_EPS)
    return (wide * inv_rms * gain).astype(BF16)


def dot_nt(a, b):
    return lax.dot_general(a, b, (((1,), (1,)), ((), ())), preferred_element_type=F32)


def layer_kernel(x_hbm, idx_ref, slot_ref, gate_ref, again_ref, mgain_ref, cos_hbm, sin_hbm, wqkv_hbm, wo_hbm, wg_hbm, wu_hbm, wd_hbm, out_ref,
                 x, cos, sin, normed, qkv, ctx, h, u, dest, dcol, gcol,
                 send, recv, ybuf, back, wqkv, wo, wg, wu, wd, act,
                 x_sem, t_sem, w_local, w_send, w_recv, out_send, out_recv, ret_send, ret_recv):
    fs = lax.axis_index('fsdp')
    ep = lax.axis_index('ep')
    me = (lax.rem(ep, 4), lax.rem(ep // 4, 4), ep // 16)
    half = D // 2

    def peer(k, sign):
        offs = (lax.rem(k, 4), lax.rem(k // 4, 4), k // 16)
        px, py, pz = [lax.rem(m + sign * o + 4, 4) for m, o in zip(me, offs)]
        return pz * 16 + py * 4 + px

    def slot_ids(k_of_row, c_of_row):
        ex = (me[0] + k_of_row) & 3
        ey = (me[1] + (k_of_row >> 2)) & 3
        ez = (me[2] + (k_of_row >> 4)) & 3
        return (ez * 16 + ey * 4 + ex) * CAP + c_of_row

    barrier = pltpu.get_barrier_semaphore()
    pl.semaphore_signal(barrier, inc=1, device_id=(0, 1 - fs, ep), device_id_type=MESH)

    @pl.loop(1, N_EP)
    def _(k):
        pl.semaphore_signal(barrier, inc=1, device_id=(0, fs, peer(k, 1)), device_id_type=MESH)

    x_copies = [pltpu.make_async_copy(x_hbm.at[pl.ds(b * SEQ, SEQ)], x.at[pl.ds(b * SEQ, SEQ)], x_sem.at[b]) for b in range(SEQS)]
    table_copies = [pltpu.make_async_copy(src, dst, t_sem.at[i]) for i, (src, dst) in enumerate(((cos_hbm, cos), (sin_hbm, sin)))]
    lo = pl.ds(pl.multiple_of(fs * half, half), half)
    weight_views = (
        (wqkv_hbm, wqkv.at[:, lo]),
        (wo_hbm, wo.at[lo]),
        (wg_hbm.at[0], wg.at[lo]),
        (wu_hbm.at[0], wu.at[lo]),
        (wd_hbm.at[0], wd.at[:, lo]),
    )
    local_copies = [pltpu.make_async_copy(src, dst, w_local.at[i]) for i, (src, dst) in enumerate(weight_views)]
    remote_copies = [
        pltpu.make_async_remote_copy(src_ref=src, dst_ref=dst, send_sem=w_send.at[i], recv_sem=w_recv.at[i], device_id=(0, 1 - fs, ep), device_id_type=MESH)
        for i, (src, dst) in enumerate(weight_views)
    ]
    x_copies[0].start()
    local_copies[0].start()
    for copy in x_copies[1:] + table_copies + local_copies[1:]:
        copy.start()

    def out_copy(k):
        rows = rows_at(k, CAP)
        return pltpu.make_async_remote_copy(
            src_ref=send.at[rows], dst_ref=recv.at[rows], send_sem=out_send.at[k], recv_sem=out_recv.at[k],
            device_id=(0, fs, peer(k, 1)), device_id_type=MESH)

    def ret_copy(k):
        rows = rows_at(k, CAP)
        return pltpu.make_async_remote_copy(
            src_ref=ybuf.at[rows], dst_ref=back.at[rows], send_sem=ret_send.at[k], recv_sem=ret_recv.at[k],
            device_id=(0, fs, peer(k, -1)), device_id_type=MESH)

    def each(g, act_on):
        for j in range(GROUP):
            k = g * GROUP + j
            if j == 0:
                pl.when(k > 0)(functools.partial(act_on, k))
            else:
                act_on(k)

    pl.semaphore_wait(barrier, N_EP)
    for copy in remote_copies:
        copy.start()

    dest[...] = jnp.where(slot_ref[...] >= 0, idx_ref[...] * CAP + slot_ref[...], -1)
    for i in range(TOK // LANES):
        b, c = divmod(i * LANES, SEQ)
        dcol[pl.ds(i * LANES, LANES)] = jnp.broadcast_to(dest[:, i * LANES:(i + 1) * LANES], (LANES, LANES)).T
        gcol[pl.ds(i * LANES, LANES)] = jnp.broadcast_to(gate_ref[b:b + 1, c:c + LANES].astype(F32), (LANES, LANES)).T

    again = again_ref[...].astype(F32)
    mgain = mgain_ref[...].astype(F32)
    for b in range(SEQS):
        x_copies[b].wait()
        normed[pl.ds(b * SEQ, SEQ)] = norm(x[pl.ds(b * SEQ, SEQ)].astype(F32), again)
    for copy in table_copies:
        copy.wait()

    local_copies[0].wait()
    remote_copies[0].wait_recv()

    lane = lax.broadcasted_iota(jnp.int32, (1, LANES), 1)
    low_half = (lane & (HEAD - 1)) < HEAD // 2
    first_head = lane < HEAD
    causal = lax.broadcasted_iota(jnp.int32, (QTILE, QTILE), 0) >= lax.broadcasted_iota(jnp.int32, (QTILE, QTILE), 1)

    @pl.loop(0, SEQS)
    def _(b):
        toks = rows_at(b, SEQ)

        @pl.loop(0, 2 * HEADS * HEAD // 256)
        def _(t):
            part = dot_nt(normed[toks], wqkv[rows_at(t, 256)])
            scale = jnp.where(t < HEADS * HEAD // 256, HEAD ** -0.5, 1.0).astype(F32)
            for j in range(256 // LANES):
                v = part[:, j * LANES:(j + 1) * LANES]
                swapped = jnp.where(low_half, pltpu.roll(v, LANES - HEAD // 2, 1), pltpu.roll(v, HEAD // 2, 1))
                rot = (v * cos[...] + swapped * sin[...]) * scale
                qkv[:, rows_at(t * 2 + j, LANES)] = rot.astype(BF16)

        @pl.loop(2 * HEADS * HEAD // 256, QKV // 256)
        def _(t):
            qkv[:, rows_at(t, 256)] = dot_nt(normed[toks], wqkv[rows_at(t, 256)]).astype(BF16)

        @pl.loop(0, HEADS // 2)
        def _(p):
            q_cols, k_cols, v_cols = [rows_at(p + i * (HEADS // 2), LANES) for i in range(3)]
            for i in range(SEQ // QTILE):
                q_pair = qkv[pl.ds(i * QTILE, QTILE), q_cols]
                outs = []
                for head_lanes in (first_head, jnp.logical_not(first_head)):
                    q = jnp.where(head_lanes, q_pair, jnp.zeros((), BF16))
                    scores = [dot_nt(q, qkv[pl.ds(j * QTILE, QTILE), k_cols]) for j in range(i + 1)]
                    scores[i] = jnp.where(causal, scores[i], -1e30)
                    top = functools.reduce(jnp.maximum, [jnp.max(s, axis=-1, keepdims=True) for s in scores])
                    exps = [jnp.exp(s - top) for s in scores]
                    inv = 1.0 / sum(jnp.sum(e, axis=-1, keepdims=True) for e in exps)
                    outs.append(sum(
                        jnp.dot((e * inv).astype(BF16), qkv[pl.ds(j * QTILE, QTILE), v_cols], preferred_element_type=F32)
                        for j, e in enumerate(exps)))
                ctx[pl.ds(i * QTILE, QTILE), rows_at(p, LANES)] = jnp.where(first_head, outs[0], outs[1]).astype(BF16)

        @pl.when(b == 0)
        def _():
            local_copies[1].wait()
            remote_copies[1].wait_recv()

        attn = jnp.dot(ctx[...], wo[...], preferred_element_type=F32)
        hidden = (x[toks].astype(F32) + attn).astype(BF16)
        h[toks] = hidden
        u[toks] = norm(hidden.astype(F32), mgain)

    @pl.loop(0, N_GROUPS)
    def _(g):
        row = lax.broadcasted_iota(jnp.int32, (GROWS, 1), 0)
        sid = slot_ids(g * GROUP + (row >> 5), row & (CAP - 1))
        pick = jnp.where(sid == dest[...], 1.0, 0.0).astype(BF16)
        send[rows_at(g, GROWS)] = jnp.dot(pick, u[...], preferred_element_type=F32).astype(BF16)
        each(g, lambda k: out_copy(k).start())

    recv[pl.ds(0, CAP)] = send[pl.ds(0, CAP)]
    for copy in local_copies[2:]:
        copy.wait()
    for copy in remote_copies[2:]:
        copy.wait_recv()

    @pl.loop(0, N_GROUPS)
    def _(g):
        each(g, lambda k: out_copy(k).wait_recv())
        here = rows_at(g, GROWS)

        @pl.loop(0, FFN // FTILE)
        def _(t):
            cols = rows_at(t, FTILE)
            gate_act = jnp.dot(recv[here], wg[:, cols], preferred_element_type=F32)
            up_act = jnp.dot(recv[here], wu[:, cols], preferred_element_type=F32)
            act[:, cols] = (jax.nn.silu(gate_act) * up_act).astype(BF16)

        ybuf[here] = jnp.dot(act[...], wd[...], preferred_element_type=F32).astype(BF16)
        each(g, lambda k: ret_copy(k).start())

    back[pl.ds(0, CAP)] = ybuf[pl.ds(0, CAP)]

    def combine(g, so_far):
        each(g, lambda k: ret_copy(k).wait_recv())
        col = lax.broadcasted_iota(jnp.int32, (1, GROWS), 1)
        sid = slot_ids(g * GROUP + (col >> 5), col & (CAP - 1))

        @pl.loop(0, TOK // TTILE)
        def _(i):
            toks = rows_at(i, TTILE)
            pick = jnp.concatenate([
                jnp.where(sid[:, j * LANES:(j + 1) * LANES] == dcol[toks], gcol[toks], 0.0).astype(BF16)
                for j in range(GROWS // LANES)], axis=1)
            part = jnp.dot(pick, back[rows_at(g, GROWS)], preferred_element_type=F32)
            out_ref[toks] = (so_far[toks].astype(F32) + part).astype(BF16)

    combine(0, h)

    @pl.loop(1, N_GROUPS)
    def _(g):
        combine(g, out_ref)

    for copy in remote_copies:
        copy.wait_send()

    @pl.loop(1, N_EP)
    def _(k):
        out_copy(k).wait_send()
        ret_copy(k).wait_send()


def rope_tables():
    half = HEAD // 2
    inv_freq = np.float32(ROPE_BASE) ** (-np.arange(half, dtype=np.float32) / np.float32(half))
    angles = (np.arange(SEQ, dtype=np.float32)[:, None] * inv_freq[None, :]).astype(np.float64)
    cos, sin = np.cos(angles).astype(np.float32), np.sin(angles).astype(np.float32)
    return np.tile(cos, (1, LANES // half)), np.tile(np.concatenate([-sin, sin], axis=1), (1, LANES // HEAD))


def layer(x, idx, slot, gate, again, mgain, wqkv, wo, wg, wu, wd):
    cos, sin = rope_tables()
    vmem = pl.BlockSpec(memory_space=pltpu.VMEM)
    hbm = pl.BlockSpec(memory_space=pl.ANY)
    dma = pltpu.SemaphoreType.DMA
    slots = N_EP * CAP
    scratch = [
        ((TOK, D), BF16), ((SEQ, LANES), F32), ((SEQ, LANES), F32), ((TOK, D), BF16), ((SEQ, QKV), BF16), ((SEQ, D), BF16),
        ((TOK, D), BF16), ((TOK, D), BF16), ((1, TOK), jnp.int32), ((TOK, LANES), jnp.int32), ((TOK, LANES), F32),
        ((slots, D), BF16), ((slots, D), BF16), ((slots, D), BF16), ((slots, D), BF16),
        ((QKV, D), BF16), ((D, D), BF16), ((D, FFN), BF16), ((D, FFN), BF16), ((FFN, D), BF16), ((GROWS, FFN), BF16),
    ]
    return pl.pallas_call(
        layer_kernel,
        out_shape=jax.ShapeDtypeStruct((TOK, D), BF16),
        in_specs=[hbm] + [vmem] * 5 + [hbm] * 7,
        out_specs=vmem,
        scratch_shapes=[pltpu.VMEM(*s) for s in scratch] + [dma((SEQS,)), dma((2,)), dma((5,)), dma((5,)), dma((5,))] + [dma((N_EP,))] * 4,
        compiler_params=pltpu.CompilerParams(collective_id=1, has_side_effects=True, vmem_limit_bytes=63 << 20),
        name='layer',
    )(x, idx, slot, gate, again, mgain, cos, sin, wqkv, wo, wg, wu, wd)


def solution(mesh):
    tok_spec = P(('data', 'fsdp', 'ep'), None, None)

    def local_step(x_blk, idx_blk, slot_blk, gate_blk, attn_gain, qkv_shard, out_shard, moe_gain, gate_shard, up_shard, down_shard):
        result = layer(
            x_blk.reshape(TOK, D), idx_blk.reshape(1, TOK), slot_blk.reshape(1, TOK), gate_blk.reshape(SEQS, SEQ),
            attn_gain.reshape(1, D), moe_gain.reshape(1, D), qkv_shard.transpose(1, 2, 3, 0).reshape(QKV, D // 2), out_shard.reshape(D // 2, D),
            gate_shard, up_shard, down_shard)
        return result.reshape(x_blk.shape)

    return jax.shard_map(local_step, mesh=mesh, in_specs=(tok_spec, tok_spec, tok_spec, tok_spec, P(None), P('fsdp', None, None, None), P('fsdp', None, None), P(None), P('ep', 'fsdp', None), P('ep', 'fsdp', None), P('ep', None, 'fsdp')), out_specs=tok_spec, check_vma=False)
```

time: 212 us -> 171 us (0.81)
  the two profiles are of different devices: /device:TPU:1 before, /device:TPU:41 now
where the time goes in v2:
time: 171 us
  Pallas kernels  165 us (96%)
  local copies, waits for them, and re-layouts  5.76 us (3%)
    pallas_call x1, Pallas kernels, layer(): pl.pallas_call(layer_kernel, out_shape=jax.ShapeDtypeStruct((TOK, D), BF1...  165 us

profile of v2, /device:TPU:41, one launch (start us, length us, event | category | flops | bytes accessed | tf_op | source)
XLA Modules:
  0.0 171.0 jit_solution(4025924193583504308)
XLA Ops:
  0.0 1.3 reshape.31.again_ref
  1.3 1.3 reshape.32.mgain_ref
  2.5 165.2 %layer.1 = bf16[1536,768]{1,0:T(8,128)(2,1)} custom-call(bf16[1536,768]{1,0:T(8,128)(2,1)} %bitcast.10, s32[1,1536]{1,0:T(1,128)} %bitcast.13, s32[1,1536]{1,0:T(1,128)} %bitcast.14, bf16[3,512]{1,0:T(4,128)(2,1)} %bitcast.15, bf16[1,768]{1,0:T(2,128)(2,1)} %reshape.31.again_ref, bf16[1,768]{1,0:T(2,128)(2,1)} %reshape.32.mgain_ref, ...), custom_call_target="tpu_custom_call" | custom-call | tf_op jit(solution)/shard_map/layer/pallas_call | solution.py:266
  167.8 3.2 %copy.15 = bf16[3,512,768]{2,1,0:T(8,128)(2,1)} copy(bf16[3,512,768]{2,1,0:T(8,128)(2,1)} %bitcast.9) | data formatting | bytes 4718592

commit v3 on v2

v3 whole, which is shorter than its diff:
```python
import functools

import jax
import jax.numpy as jnp
import numpy as np
from jax import lax
from jax.experimental import pallas as pl
from jax.experimental.pallas import tpu as pltpu
from jax.sharding import PartitionSpec as P

MESH = pl.DeviceIdType.MESH
NORM_EPS = 1e-6
ROPE_BASE = 10000.0
N_EP = 64
CAP = 32
GROUP = 8
GROWS = GROUP * CAP
N_GROUPS = N_EP // GROUP
SEQS = 3
SEQ = 512
TOK = SEQS * SEQ
TTILE = 512
D = 768
FFN = 3072
FTILE = 512
STRIDE = 27
ETILE = 512
HEADS = 12
HEAD = 64
QKV = 3 * HEADS * HEAD
QTILE = 256
WTILE = 384
LANES = 128
F32, BF16 = jnp.float32, jnp.bfloat16


def rows_at(i, size):
    return pl.ds(pl.multiple_of(i * size, size), size)


def norm(wide, gain):
    inv_rms = lax.rsqrt(jnp.mean(wide * wide, axis=-1, keepdims=True) + NORM_EPS)
    return (wide * inv_rms * gain).astype(BF16)


def dot_nt(a, b):
    return lax.dot_general(a, b, (((1,), (1,)), ((), ())), preferred_element_type=F32)


def layer_kernel(x_hbm, idx_ref, slot_ref, gate_ref, again_ref, mgain_ref, cos_hbm, sin_hbm, wqkv_hbm, wo_hbm, wg_hbm, wu_hbm, wd_hbm,
                 sum_hbm, pick_hbm, last_hbm,
                 x, cos, sin, normed, qkv, ctx, h, u, dest, dcol, gcol,
                 send, recv, ybuf, back, wqkv, wo, wg, wu, wd, act, pick_last,
                 x_sem, t_sem, o_sem, w_local, w_send, w_recv, out_send, out_recv, ret_send, ret_recv):
    fs = lax.axis_index('fsdp')
    ep = lax.axis_index('ep')
    me = (lax.rem(ep, 4), lax.rem(ep // 4, 4), ep // 16)
    half = D // 2

    def peer(i, sign):
        k = lax.rem(i * STRIDE, N_EP)
        offs = (lax.rem(k, 4), lax.rem(k // 4, 4), k // 16)
        px, py, pz = [lax.rem(m + sign * o + 4, 4) for m, o in zip(me, offs)]
        return pz * 16 + py * 4 + px

    def slot_ids(i_of_row, c_of_row):
        k_of_row = (i_of_row * STRIDE) & (N_EP - 1)
        ex = (me[0] + k_of_row) & 3
        ey = (me[1] + (k_of_row >> 2)) & 3
        ez = (me[2] + (k_of_row >> 4)) & 3
        return (ez * 16 + ey * 4 + ex) * CAP + c_of_row

    barrier = pltpu.get_barrier_semaphore()
    pl.semaphore_signal(barrier, inc=1, device_id=(0, 1 - fs, ep), device_id_type=MESH)

    @pl.loop(1, N_EP)
    def _(k):
        pl.semaphore_signal(barrier, inc=1, device_id=(0, fs, peer(k, 1)), device_id_type=MESH)

    x_copies = [pltpu.make_async_copy(x_hbm.at[pl.ds(b * SEQ, SEQ)], x.at[pl.ds(b * SEQ, SEQ)], x_sem.at[b]) for b in range(SEQS)]
    table_copies = [pltpu.make_async_copy(src, dst, t_sem.at[i]) for i, (src, dst) in enumerate(((cos_hbm, cos), (sin_hbm, sin)))]
    lo = pl.ds(pl.multiple_of(fs * half, half), half)
    weight_views = (
        (wqkv_hbm, wqkv.at[:, lo]),
        (wo_hbm, wo.at[lo]),
        (wg_hbm.at[0], wg.at[lo]),
        (wu_hbm.at[0], wu.at[lo]),
        (wd_hbm.at[0], wd.at[:, lo]),
    )
    local_copies = [pltpu.make_async_copy(src, dst, w_local.at[i]) for i, (src, dst) in enumerate(weight_views)]
    remote_copies = [
        pltpu.make_async_remote_copy(src_ref=src, dst_ref=dst, send_sem=w_send.at[i], recv_sem=w_recv.at[i], device_id=(0, 1 - fs, ep), device_id_type=MESH)
        for i, (src, dst) in enumerate(weight_views)
    ]
    x_copies[0].start()
    local_copies[0].start()
    for copy in x_copies[1:] + table_copies + local_copies[1:]:
        copy.start()

    def out_copy(k):
        rows = rows_at(k, CAP)
        return pltpu.make_async_remote_copy(
            src_ref=send.at[rows], dst_ref=recv.at[rows], send_sem=out_send.at[k], recv_sem=out_recv.at[k],
            device_id=(0, fs, peer(k, 1)), device_id_type=MESH)

    def ret_copy(k, last=False):
        rows = rows_at(k, CAP)
        landing = last_hbm.at[rows_at(k - (N_EP - GROUP), CAP)] if last else back.at[rows]
        return pltpu.make_async_remote_copy(
            src_ref=ybuf.at[rows], dst_ref=landing, send_sem=ret_send.at[k], recv_sem=ret_recv.at[k],
            device_id=(0, fs, peer(k, -1)), device_id_type=MESH)

    def each(g, act_on):
        for j in range(GROUP):
            k = g * GROUP + j
            if j == 0:
                pl.when(k > 0)(functools.partial(act_on, k))
            else:
                act_on(k)

    with jax.named_scope('tables'):
        dest[...] = jnp.where(slot_ref[...] >= 0, idx_ref[...] * CAP + slot_ref[...], -1)
        for i in range(TOK // LANES):
            b, c = divmod(i * LANES, SEQ)
            dcol[pl.ds(i * LANES, LANES)] = jnp.broadcast_to(dest[:, i * LANES:(i + 1) * LANES], (LANES, LANES)).T
            gcol[pl.ds(i * LANES, LANES)] = jnp.broadcast_to(gate_ref[b:b + 1, c:c + LANES].astype(F32), (LANES, LANES)).T
    again = again_ref[...].astype(F32).reshape(1, D)
    mgain = mgain_ref[...].astype(F32).reshape(1, D)
    with jax.named_scope('norm_in'):
        for b in range(SEQS):
            x_copies[b].wait()
            normed[pl.ds(b * SEQ, SEQ)] = norm(x[pl.ds(b * SEQ, SEQ)].astype(F32), again)
    with jax.named_scope('barrier'):
        pl.semaphore_wait(barrier, N_EP)
    for copy in remote_copies:
        copy.start()

    for copy in table_copies:
        copy.wait()

    with jax.named_scope('wqkv_wait'):
        local_copies[0].wait()
        remote_copies[0].wait_recv()

    first_head = lax.broadcasted_iota(jnp.int32, (1, LANES), 1) < HEAD
    causal = lax.broadcasted_iota(jnp.int32, (QTILE, QTILE), 0) <= lax.broadcasted_iota(jnp.int32, (QTILE, QTILE), 1)

    @pl.loop(0, SEQS)
    def _(b):
        toks = rows_at(b, SEQ)

        with jax.named_scope('qk'):
            @pl.loop(0, 2 * HEADS * HEAD // WTILE)
            def _(t):
                part = dot_nt(wqkv[rows_at(t, WTILE)], normed[toks])
                which = t // (HEADS * HEAD // WTILE)
                c, s = cos[which], sin[which]
                for j in range(WTILE // HEAD):
                    first, second = part[j * HEAD:j * HEAD + HEAD // 2], part[j * HEAD + HEAD // 2:(j + 1) * HEAD]
                    qkv[pl.ds(pl.multiple_of(t * WTILE + j * HEAD, HEAD), HEAD // 2)] = (first * c - second * s).astype(BF16)
                    qkv[pl.ds(pl.multiple_of(t * WTILE + j * HEAD + HEAD // 2, HEAD // 2), HEAD // 2)] = (second * c + first * s).astype(BF16)

        with jax.named_scope('v'):
            @pl.loop(2 * HEADS * HEAD // WTILE, QKV // WTILE)
            def _(t):
                qkv[rows_at(t, WTILE)] = dot_nt(wqkv[rows_at(t, WTILE)], normed[toks]).astype(BF16)

        with jax.named_scope('attn'):
            @pl.loop(0, HEADS // 2)
            def _(p):
                q_rows, k_rows = rows_at(p, LANES), rows_at(p + HEADS // 2, LANES)
                k_pair = qkv[k_rows].T
                for hh in range(2):
                    k = jnp.where(first_head if hh == 0 else jnp.logical_not(first_head), k_pair, jnp.zeros((), BF16))
                    v = qkv[pl.ds(pl.multiple_of(2 * HEADS * HEAD + p * LANES + hh * HEAD, HEAD), HEAD)]
                    for i in range(SEQ // QTILE):
                        scores = [jnp.dot(k[j * QTILE:(j + 1) * QTILE], qkv[q_rows, pl.ds(i * QTILE, QTILE)], preferred_element_type=F32) for j in range(i + 1)]
                        scores[i] = jnp.where(causal, scores[i], -1e30)
                        top = functools.reduce(jnp.maximum, [jnp.max(s, axis=0, keepdims=True) for s in scores])
                        exps = [jnp.exp(s - top) for s in scores]
                        inv = 1.0 / sum(jnp.sum(e, axis=0, keepdims=True) for e in exps)
                        out = sum(
                            jnp.dot(v[:, j * QTILE:(j + 1) * QTILE], (e * inv).astype(BF16), preferred_element_type=F32)
                            for j, e in enumerate(exps))
                        ctx[pl.ds(pl.multiple_of(p * LANES + hh * HEAD, HEAD), HEAD), pl.ds(i * QTILE, QTILE)] = out.astype(BF16)

        @pl.when(b == 0)
        def _():
            local_copies[1].wait()
            remote_copies[1].wait_recv()

        with jax.named_scope('proj'):
            attn = lax.dot_general(ctx[...], wo[...], (((0,), (0,)), ((), ())), preferred_element_type=F32)
            hidden = (x[toks].astype(F32) + attn).astype(BF16)
            h[toks] = hidden
            u[toks] = norm(hidden.astype(F32), mgain)
    @pl.loop(0, N_GROUPS)
    def _(g):
        with jax.named_scope('dispatch'):
            row = lax.broadcasted_iota(jnp.int32, (GROWS, 1), 0)
            sid = slot_ids(g * GROUP + (row >> 5), row & (CAP - 1))
            pick = jnp.where(sid == dest[...], 1.0, 0.0).astype(BF16)
            send[rows_at(g, GROWS)] = jnp.dot(pick, u[...], preferred_element_type=F32).astype(BF16)
            each(g, lambda k: out_copy(k).start())
    recv[pl.ds(0, CAP)] = send[pl.ds(0, CAP)]
    with jax.named_scope('w_wait'):
        for copy in local_copies[2:]:
            copy.wait()
        for copy in remote_copies[2:]:
            copy.wait_recv()
    def experts(g, last=False):
        with jax.named_scope('ffn_wait'):
            each(g, lambda k: out_copy(k).wait_recv())
        here = rows_at(g, GROWS)

        with jax.named_scope('ffn_up'):
            @pl.loop(0, FFN // FTILE)
            def _(t):
                cols = rows_at(t, FTILE)
                gate_act = jnp.dot(recv[here], wg[:, cols], preferred_element_type=F32)
                up_act = jnp.dot(recv[here], wu[:, cols], preferred_element_type=F32)
                act[:, cols] = (jax.nn.silu(gate_act) * up_act).astype(BF16)

        with jax.named_scope('ffn_down'):
            ybuf[here] = jnp.dot(act[...], wd[...], preferred_element_type=F32).astype(BF16)
            each(g, lambda k: ret_copy(k, last).start())

    @pl.loop(0, N_GROUPS - 1)
    def _(g):
        experts(g)

    experts(jnp.int32(N_GROUPS - 1), True)
    back[pl.ds(0, CAP)] = ybuf[pl.ds(0, CAP)]

    def pick_of(g, toks):
        col = lax.broadcasted_iota(jnp.int32, (1, GROWS), 1)
        sid = slot_ids(g * GROUP + (col >> 5), col & (CAP - 1))
        return jnp.concatenate([
            jnp.where(sid[:, j * LANES:(j + 1) * LANES] == dcol[toks], gcol[toks], 0.0).astype(BF16)
            for j in range(GROWS // LANES)], axis=1)

    pick_last[...] = pick_of(N_GROUPS - 1, pl.ds(0, TOK))
    pick_out = pltpu.make_async_copy(pick_last, pick_hbm, o_sem.at[0])
    pick_out.start()

    @pl.loop(0, N_GROUPS - 1)
    def _(g):
        with jax.named_scope('comb_wait'):
            each(g, lambda k: ret_copy(k).wait_recv())
        with jax.named_scope('comb'):
            @pl.loop(0, TOK // TTILE)
            def _(i):
                toks = rows_at(i, TTILE)
                part = jnp.dot(pick_of(g, toks), back[rows_at(g, GROWS)], preferred_element_type=F32)
                h[toks] = (h[toks].astype(F32) + part).astype(BF16)

    sum_out = pltpu.make_async_copy(h, sum_hbm, o_sem.at[1])
    sum_out.start()

    for copy in remote_copies:
        copy.wait_send()

    @pl.loop(1, N_EP)
    def _(k):
        out_copy(k).wait_send()

    @pl.loop(1, N_EP - GROUP)
    def _(k):
        ret_copy(k).wait_send()

    pick_out.wait()
    sum_out.wait()
    with jax.named_scope('last_wait'):
        @pl.loop(N_EP - GROUP, N_EP)
        def _(k):
            ret_copy(k, True).wait_recv()
            ret_copy(k, True).wait_send()


def finish_kernel(sum_ref, pick_ref, last_ref, out_ref):
    part = jnp.dot(pick_ref[...], last_ref[...], preferred_element_type=F32)
    out_ref[...] = (sum_ref[...].astype(F32) + part).astype(BF16)


def rope_tables():
    half = HEAD // 2
    inv_freq = np.float32(ROPE_BASE) ** (-np.arange(half, dtype=np.float32) / np.float32(half))
    angles = (inv_freq[:, None] * np.arange(SEQ, dtype=np.float32)[None, :]).astype(np.float64)
    scale = np.float32(HEAD ** -0.5)
    return [np.stack([table * scale, table]) for table in (np.cos(angles).astype(np.float32), np.sin(angles).astype(np.float32))]


def layer(x, idx, slot, gate, again, mgain, wqkv, wo, wg, wu, wd):
    cos, sin = rope_tables()
    vmem = pl.BlockSpec(memory_space=pltpu.VMEM)
    hbm = pl.BlockSpec(memory_space=pl.ANY)
    dma = pltpu.SemaphoreType.DMA
    slots = N_EP * CAP
    scratch = [
        ((TOK, D), BF16), ((2, HEAD // 2, SEQ), F32), ((2, HEAD // 2, SEQ), F32), ((TOK, D), BF16), ((QKV, SEQ), BF16), ((D, SEQ), BF16),
        ((TOK, D), BF16), ((TOK, D), BF16), ((1, TOK), jnp.int32), ((TOK, LANES), jnp.int32), ((TOK, LANES), F32),
        ((slots, D), BF16), ((slots, D), BF16), ((slots, D), BF16), ((slots, D), BF16),
        ((QKV, D), BF16), ((D, D), BF16), ((D, FFN), BF16), ((D, FFN), BF16), ((FFN, D), BF16), ((GROWS, FFN), BF16), ((TOK, GROWS), BF16),
    ]
    total, pick, last = pl.pallas_call(
        layer_kernel,
        out_shape=[jax.ShapeDtypeStruct((TOK, D), BF16), jax.ShapeDtypeStruct((TOK, GROWS), BF16), jax.ShapeDtypeStruct((GROWS, D), BF16)],
        in_specs=[hbm] + [vmem] * 5 + [hbm] * 7,
        out_specs=[hbm] * 3,
        scratch_shapes=[pltpu.VMEM(*s) for s in scratch] + [dma((SEQS,)), dma((2,)), dma((2,)), dma((5,)), dma((5,)), dma((5,))] + [dma((N_EP,))] * 4,
        compiler_params=pltpu.CompilerParams(collective_id=1, has_side_effects=True, vmem_limit_bytes=63 << 20),
        name='layer',
    )(x, idx, slot, gate, again, mgain, cos, sin, wqkv, wo, wg, wu, wd)
    return pl.pallas_call(
        finish_kernel,
        grid=(TOK // ETILE,),
        out_shape=jax.ShapeDtypeStruct((TOK, D), BF16),
        in_specs=[pl.BlockSpec((ETILE, D), lambda i: (i, 0)), pl.BlockSpec((ETILE, GROWS), lambda i: (i, 0)), pl.BlockSpec((GROWS, D), lambda i: (0, 0))],
        out_specs=pl.BlockSpec((ETILE, D), lambda i: (i, 0)),
        name='finish',
    )(total, pick, last)


def solution(mesh):
    tok_spec = P(('data', 'fsdp', 'ep'), None, None)

    def local_step(x_blk, idx_blk, slot_blk, gate_blk, attn_gain, qkv_shard, out_shard, moe_gain, gate_shard, up_shard, down_shard):
        result = layer(
            x_blk.reshape(TOK, D), idx_blk.reshape(1, TOK), slot_blk.reshape(1, TOK), gate_blk.reshape(SEQS, SEQ),
            attn_gain, moe_gain, qkv_shard.transpose(1, 2, 3, 0).reshape(QKV, D // 2), out_shard.reshape(D // 2, D),
            gate_shard, up_shard, down_shard)
        return result.reshape(x_blk.shape)

    return jax.shard_map(local_step, mesh=mesh, in_specs=(tok_spec, tok_spec, tok_spec, tok_spec, P(None), P('fsdp', None, None, None), P('fsdp', None, None), P(None), P('ep', 'fsdp', None), P('ep', 'fsdp', None), P('ep', None, 'fsdp')), out_specs=tok_spec, check_vma=False)
```

time: 171 us -> 157 us (0.918)
  the two profiles are of different devices: /device:TPU:41 before, /device:TPU:97 now
where the time goes in v3:
time: 157 us
  Pallas kernels  156 us (99%)
    pallas_call x1, Pallas kernels, layer(): pl.pallas_call(layer_kernel, out_shape=[jax.ShapeDtypeStruct((TOK, D), BF...  152 us
    pallas_call x1, Pallas kernels, layer(): pl.pallas_call(finish_kernel, grid=(TOK // ETILE,), out_shape=jax.ShapeDt...  4.96 us

profile of v3, /device:TPU:97, one launch (start us, length us, event | category | flops | bytes accessed | tf_op | source)
XLA Modules:
  0.0 156.5 jit_solution(2405813716161912045)
XLA Ops:
  0.0 151.5 %layer.1 = (bf16[1536,768]{1,0:T(8,128)(2,1)}, bf16[1536,256]{1,0:T(8,128)(2,1)}, bf16[256,768]{1,0:T(8,128)(2,1)}) custom-call(bf16[1536,768]{1,0:T(8,128)(2,1)} %bitcast.9, s32[1,1536]{1,0:T(1,128)} %bitcast.12, s32[1,1536]{1,0:T(1,128)} %bitcast.13, bf16[3,512]{1,0:T(4,128)(2,1)} %bitcast.14, bf16[768]{0:T(1024)(128)(2,1)} %again_ref.1, ...), custom_call_target="tpu_custom_call" | custom-call | tf_op jit(solution)/shard_map/layer/pallas_call | solution.py:305
  151.6 5.0 %finish.1 = bf16[1536,768]{1,0:T(8,128)(2,1)} custom-call(bf16[1536,768]{1,0:T(8,128)(2,1)} %get-tuple-element.8.sum_ref, bf16[1536,256]{1,0:T(8,128)(2,1)} %get-tuple-element.9.pick_ref, bf16[256,768]{1,0:T(8,128)(2,1)} %get-tuple-element.10.last_ref), custom_call_target="tpu_custom_call" | custom-call | tf_op jit(solution)/shard_map/finish/pallas_call | solution.py:314
